TPU v7x, 32 devices: a whole 2x2x4 slice. The times are simulated.
32 devices in a mesh: tok: 8 (over y, x, core), exp: 4 (over z).
Axes of the slice: x: 2, y: 2, z: 4, core: 2. Of those that a mesh axis runs over, the one named last changes fastest.
Arguments:
- expert_rows: bfloat16 [4, 2048, 4096], P('exp', 'tok'), may hold values from -480 to 480
- router_input: bfloat16 [2048, 4096], P(('tok', 'exp')), may hold values from -6 to 6
- router_weight: float32 [4096, 4], replicated, may hold values from -0.09375 to 0.09375
- assign: int32 [2048, 2], P(('tok', 'exp')), may hold values from 0 to 3, all different within a row
- targets: int32 [2048], P(('tok', 'exp')), may hold values from 0 to 15999
- head: bfloat16 [4096, 16000], P('tok', 'exp'), may hold values from -0.35 to 0.35
Outputs:
- token_loss: float32 [2048], P(('tok', 'exp'))
- router_grad: float32 [4096, 4], replicated
- mean_loss: float32 [], replicated
All inputs are finite; a program needn't handle non-finite values.
Results may differ from a plain program's by a relative error of at most 0.007.
Values may be sent and summed in bfloat16 or wider, within the bound.
A program may use at most 128 MiB of HBM per device.

v0:
```python
import math
import jax
import jax.numpy as jnp
from jax import lax
from jax.sharding import PartitionSpec as P


def shards(expert_rows, router_input, router_weight, assign, targets, head):
    experts = router_weight.shape[1]
    own_rows = router_input.shape[0]
    tokens_all = own_rows * lax.axis_size("tok") * lax.axis_size("exp")
    loss_scale = 1.0 / math.sqrt(tokens_all)
    inputs = router_input.astype(jnp.float32)
    gate_logits = jnp.dot(inputs, router_weight, precision=lax.Precision.HIGHEST)
    labels = jnp.arange(experts, dtype=jnp.int32)
    first_hot = (assign[:, 0:1] == labels[None, :]).astype(jnp.float32)
    second_hot = (assign[:, 1:2] == labels[None, :]).astype(jnp.float32)
    differ = first_hot - second_hot
    mix_share = jax.nn.sigmoid(jnp.sum(gate_logits * differ, axis=1))
    mixing = mix_share[:, None] * first_hot + (1.0 - mix_share)[:, None] * second_hot
    local_rows = lax.all_to_all(expert_rows, "exp", split_axis=1, concat_axis=0, tiled=True)
    local_wide = local_rows.astype(jnp.float32)
    mixed_own = jnp.sum(mixing.T[:, :, None] * local_wide, axis=0).astype(jnp.bfloat16)
    mixed_rows, group_targets = (
        lax.all_gather(mixed_own, "exp", axis=0, tiled=True),
        lax.all_gather(targets, "exp", axis=0, tiled=True),
    )
    shard_width = head.shape[1]
    full_head = lax.all_gather(head, "tok", axis=0, tiled=True)
    logits = jnp.dot(mixed_rows, full_head, preferred_element_type=jnp.float32)
    first_col = lax.axis_index("exp") * shard_width
    columns = first_col + jnp.arange(shard_width, dtype=jnp.int32)
    target_hit = group_targets[:, None] == columns[None, :]
    picked = jnp.sum(jnp.where(target_hit, logits, 0.0), axis=1)
    local_top = jnp.max(logits, axis=1)
    row_top = lax.pmax(local_top, "exp")
    exp_total, target_logit = lax.psum(
        (jnp.sum(jnp.exp(logits - row_top[:, None]), axis=1), picked), "exp"
    )
    log_total = row_top + jnp.log(exp_total)
    group_loss = log_total - target_logit
    own_loss = lax.dynamic_slice_in_dim(group_loss, lax.axis_index("exp") * own_rows, own_rows, 0)
    loss_sum = lax.psum(jnp.sum(own_loss), ("tok", "exp"))
    slope = (
        loss_scale * (jnp.exp(logits - log_total[:, None]) - target_hit.astype(jnp.float32))
    ).astype(jnp.bfloat16)
    hidden_slope = lax.psum_scatter(
        lax.dot_general(
            slope, full_head, (((1,), (1,)), ((), ())), preferred_element_type=jnp.float32
        ).astype(jnp.bfloat16),
        "exp",
        scatter_dimension=0,
        tiled=True,
    ).astype(jnp.float32)
    weight_slope = jnp.sum(hidden_slope[None, :, :] * local_wide, axis=2).T
    spread = jnp.sum(weight_slope * differ, axis=1) * mix_share * (1.0 - mix_share)
    gate_slope = spread[:, None] * differ
    router_part = jnp.dot(inputs.T, gate_slope, precision=lax.Precision.HIGHEST)
    router_sum = lax.psum(router_part, ("tok", "exp"))
    mean_loss = loss_sum / tokens_all
    return (own_loss, router_sum, mean_loss)


def solution(mesh):
    in_specs = (
        P("exp", "tok", None),
        P(("tok", "exp"), None),
        P(),
        P(("tok", "exp"), None),
        P(("tok", "exp")),
        P("tok", "exp"),
    )
    out_specs = (P(("tok", "exp")), P(), P())
    return jax.shard_map(shards, mesh=mesh, in_specs=in_specs, out_specs=out_specs, check_vma=False)
```

profile of v0, /device:TPU:1, one launch (start us, length us, event | category | flops | bytes accessed | tf_op | source)
XLA Modules:
  0.0 542.0 jit_solution(5459968139769704115)
XLA Ops:
  7.2 8.4 %copy.16 = bf16[1,256,4096]{2,0,1:T(2,128)(2,1)} copy(bf16[1,256,4096]{2,1,0:T(8,128)(2,1)} %param.6) | data formatting | bytes 4194304 | tf_op args[0]
  16.1 13.5 %reduce.1 = bf16[256,4096]{1,0:T(8,128)(2,1)S(1)} reduce(bf16[256,1,4096]{2,1,0:T(2,128)(2,1)} %bitcast.29, bf16[]{:T(256)} %broadcast.107), dimensions={1}, to_apply=%bitcast.25.reduce_sub_computation | reduce | bytes 4194306
  29.6 2.8 reshape.110
  32.4 5.4 all-to-all-start
  38.4 47.2 %all-to-all-done = bf16[4,2,131072]{2,1,0:T(2,128)(2,1)S(1)} async-done(((bf16[4,2,131072]{2,1,0:T(2,128)(2,1)}), bf16[4,2,131072]{2,1,0:T(2,128)(2,1)S(1)}, u32[]{:S(2)}, u32[]{:S(2)}) %all-to-all-start) | async-done | bytes 2097184 | tf_op jit(solution)/shard_map/all_to_all | solution.py:21
  85.6 3.3 reshape.111
  88.9 6.0 %copy_convert_fusion = f32[1,256,4096]{2,1,0:T(8,128)S(1)} fusion(bf16[1,256,4096]{2,0,1:T(2,128)(2,1)} %bitcast.27), kind=kLoop, calls=%fused_computation.12 | loop fusion | flops 1048576 | bytes 6291456 | tf_op jit(solution)/shard_map/convert_element_type | solution.py:22
  94.9 1.4 multiply_reduce_fusion
  98.8 4.0 all-reduce
  102.8 39.0 %all-gather.3.cloned.1.call-done = bf16[256,4096]{1,0:T(8,128)(2,1)} async-done(((bf16[64,4096]{1,0:T(8,128)(2,1)}), bf16[256,4096]{1,0:T(8,128)(2,1)}) %all-gather.3.cloned.1.call-update) | async-done | bytes 2097168 | tf_op jit(solution)/shard_map/all_gather | solution.py:25
  141.8 165.1 %all-gather.5.cloned.1.call-done = bf16[4096,4000]{0,1:T(8,128)(2,1)} async-done(((bf16[512,4000]{0,1:T(8,128)(2,1)}), bf16[4096,4000]{0,1:T(8,128)(2,1)}) %all-gather.5.cloned.1.call-update) | async-done | bytes 32768016 | tf_op jit(solution)/shard_map/all_gather | solution.py:29
  306.9 16.2 %fusion.19 = (f32[256]{0:T(256)S(1)}, f32[256,4000]{0,1:T(8,128)}) fusion(bf16[256,4096]{1,0:T(8,128)(2,1)} %all-gather.3.cloned.1.call-done, bf16[4096,4000]{0,1:T(8,128)(2,1)} %all-gather.5.cloned.1.call-done), kind=kOutput, calls=%fused_computation.41 | convolution fusion | flops 8389632000 | bytes 38962176 | tf_op jit(solution)/shard_map/dot_general | solution.py:30
  323.2 9.7 %pmax.7 = f32[256]{0:T(256)S(1)} all-reduce(f32[256]{0:T(256)S(1)} %get-tuple-element.15), channel_id=1, replica_groups=mesh['tok'=8,'exp'=4] {'exp'}, use_global_device_ids=true, to_apply=%region_3.4 | all-reduce | flops 256 | bytes 2048 | tf_op jit(solution)/shard_map/pmax | solution.py:36
  332.8 3.9 fusion.1
  336.7 6.6 %all-reduce.1 = (f32[256]{0:T(256)S(1)}, f32[256]{0:T(256)S(1)}) all-reduce(f32[256]{0:T(256)S(1)} %get-tuple-element.4, f32[256]{0:T(256)S(1)} %get-tuple-element.3), channel_id=1, replica_groups=mesh['tok'=8,'exp'=4] {'exp'}, use_global_device_ids=true, to_apply=%region_5.6 | all-reduce | flops 512 | bytes 4096 | tf_op jit(solution)/shard_map/psum | solution.py:37
  343.3 17.2 %convolution_convert_fusion = bf16[256,4096]{1,0:T(8,128)(2,1)} fusion(bf16[4096,4000]{0,1:T(8,128)(2,1)} %all-gather.5.cloned.1.call-done, f32[256,4000]{0,1:T(8,128)} %get-tuple-element.16, f32[256]{0:T(256)S(1)} %get-tuple-element.10, s32[256]{0:T(256)S(1)} %all-reduce, s32[4000]{0:T(1024)S(1)} %iota_add_fusion), kind=kOutput, calls=%fused_computation | convolution fusion | flops 8395800576 | bytes 38979200 | tf_op jit(solution)/shard_map/dot_general | solution.py:48
  360.6 45.4 %reduce-scatter.2.cloned.1.call-done = bf16[64,4096]{1,0:T(8,128)(2,1)} async-done(((bf16[256,4096]{1,0:T(8,128)(2,1)}), bf16[64,4096]{1,0:T(8,128)(2,1)}) %reduce-scatter.2.cloned.1.call-update) | async-done | bytes 524304 | tf_op jit(solution)/shard_map/reduce_scatter | solution.py:47
  406.0 1.7 mul.89
  408.3 2.4 fusion
  410.8 1.0 convolution_bitcast_fusion
  411.8 1.2 fusion.17
  413.0 39.8 %psum.31 = f32[]{:T(128)} all-reduce(f32[]{:T(128)} %get-tuple-element.7), channel_id=1, replica_groups=mesh['tok'=8,'exp'=4] {'tok','exp'}, use_global_device_ids=true, to_apply=%region_13.14 | all-reduce | flops 1 | bytes 8 | tf_op jit(solution)/shard_map/psum | solution.py:43
  453.4 79.5 %all-reduce.4.cloned.1.call-done = f32[4096,4]{0,1:T(4,128)} async-done(((f32[4096,4]{0,1:T(4,128)}), f32[4096,4]{0,1:T(4,128)}) %all-reduce.4.cloned.1.call-update) | async-done | bytes 65552 | tf_op jit(solution)/shard_map/psum | solution.py:59
  532.9 1.5 copy.19
  (33 shorter events, 3.8 us)
Async XLA Ops:
  7.2 30.7 %copy-start = (bf16[64,4096]{1,0:T(8,128)(2,1)S(1)}, bf16[64,4096]{1,0:T(8,128)(2,1)}, u32[]{:S(2)}) copy-start(bf16[64,4096]{1,0:T(8,128)(2,1)} %param.7) | copy-start | bytes 1572868
  29.6 8.2 %copy-start.3 = (s32[64,2]{0,1:T(2,128)S(1)}, s32[64,2]{0,1:T(2,128)}, u32[]{:S(2)}) copy-start(s32[64,2]{0,1:T(2,128)} %param.9) | copy-start | bytes 1540
  29.6 8.2 %copy-start.2 = (f32[4096,4]{0,1:T(4,128)S(1)}, f32[4096,4]{0,1:T(4,128)}, u32[]{:S(2)}) copy-start(f32[4096,4]{0,1:T(4,128)} %param.8) | copy-start | bytes 196612
  32.4 53.2 %all-to-all-start = ((bf16[4,2,131072]{2,1,0:T(2,128)(2,1)}), bf16[4,2,131072]{2,1,0:T(2,128)(2,1)S(1)}, u32[]{:S(2)}, u32[]{:S(2)}) async-start(bf16[4,2,131072]{2,1,0:T(2,128)(2,1)} %reshape.110), calls=%async_computation | async-start | bytes 4194304 | tf_op jit(solution)/shard_map/all_to_all | solution.py:21
  37.8 104.0 %all-gather.3.cloned.1.call-start = ((), (), s32[]{:S(2)}) async-start(), calls=%async_computation.2 | async-start | bytes 2621440 | tf_op jit(solution)/shard_map/all_gather | solution.py:25
  94.9 2.4 copy-start.5
  94.9 3.6 copy-start.4
  96.3 210.6 %all-gather.5.cloned.1.call-start = ((), (), s32[]{:S(2)}) async-start(), calls=%async_computation.3 | async-start | bytes 36864000 | tf_op jit(solution)/shard_map/all_gather | solution.py:29
  97.1 308.9 %reduce-scatter.2.cloned.1.call-start = ((), (), s32[]{:S(2)}) async-start(), calls=%async_computation.4 | async-start | bytes 2621440 | tf_op jit(solution)/shard_map/reduce_scatter | solution.py:47
  360.5 172.3 %all-reduce.4.cloned.1.call-start = ((), (), s32[]{:S(2)}) async-start(), calls=%async_computation.5 | async-start | bytes 131072 | tf_op jit(solution)/shard_map/psum | solution.py:59
  406.0 2.3 copy-start.1
Sparse Core Ops, SparseCore 0:
  96.4 45.3 all-gather.2
  143.6 163.2 all-gather.4
  360.7 45.2 reduce-scatter.1
  412.0 120.8 all-reduce.3
where the time goes:
time: 543 us; the launch traced here: 542 us
  waiting for transfers between devices  377 us (69%)
  blocking collectives  60.1 us (11%)
  matrix products  34.9 us (6%)
  other arithmetic  28.4 us (5%)
  local copies, waits for them, and re-layouts  19.7 us (4%)
  between operations  16.3 us (3%)
  starting transfers between devices  5.71 us (1%)
    all_gather x1, waiting for transfers between devices, shards(): full_head = lax.all_gather(head, 'tok', axis=0, tiled=True)  165 us
    psum x1, waiting for transfers between devices, shards(): router_sum = lax.psum(router_part, ('tok', 'exp'))  79.5 us
    all_to_all x1, waiting for transfers between devices, shards(): lax.all_to_all(expert_rows, 'exp', split_axis=1, concat_axis=0, tiled=True)  47.2 us
    reduce_scatter x1, waiting for transfers between devices, shards(): lax.psum_scatter(lax.dot_general(slope, full_head, (((1,), (1,)), ((), ()...  45.4 us
    psum x1, blocking collectives, shards(): loss_sum = lax.psum(jnp.sum(own_loss), ('tok', 'exp'))  39.8 us
    all_gather x1, waiting for transfers between devices, shards(): lax.all_gather(mixed_own, 'exp', axis=0, tiled=True)  39 us
    unnamed x20, local copies, waits for them, and re-layouts  18 us
    dot_general x1, matrix products, shards(): lax.dot_general(slope, full_head, (((1,), (1,)), ((), ())), preferred_ele...  17.2 us
  transfers between devices with their start and end apart: 5, of which 5 were waited for; matrix products, arithmetic and copies ran while one was open for 0% of the time, Pallas kernels for 0%

commit v1 on v0

--- a/solution.py
+++ b/solution.py
@@ -26,7 +26,12 @@
         lax.all_gather(targets, "exp", axis=0, tiled=True),
     )
     shard_width = head.shape[1]
-    full_head = lax.all_gather(head, "tok", axis=0, tiled=True)
+    ring = [head]
+    for hop in range(7):
+        ring.append(lax.ppermute(ring[-1], "tok", [(dev, (dev + 1) % 8) for dev in range(8)]))
+    full_head = jnp.roll(
+        jnp.concatenate(ring[::-1], axis=0), (lax.axis_index("tok") + 1) * ring[0].shape[0], axis=0
+    )
     logits = jnp.dot(mixed_rows, full_head, preferred_element_type=jnp.float32)
     first_col = lax.axis_index("exp") * shard_width
     columns = first_col + jnp.arange(shard_width, dtype=jnp.int32)

time: 543 us -> 644 us (1.19)
  local copies, waits for them, and re-layouts: 19.7 us -> 82.3 us
  blocking collectives: 60.1 us -> 85.7 us
  starting transfers between devices: 5.71 us -> 22.4 us
    ppermute x0 -> x7, waiting for transfers between devices: none -> 240 us  [shards(): lax.ppermute(ring[-1], 'tok', [(dev, (dev + 1) % 8) for dev in range(8)])]
    all_gather x1 -> x0, waiting for transfers between devices: 165 us -> none  [shards(): full_head = lax.all_gather(head, 'tok', axis=0, tiled=True)]
    unnamed x20 -> x53, local copies, waits for them, and re-layouts: 18 us -> 78.3 us
    all_to_all x1, waiting for transfers between devices: 47.2 us -> 0.01 us  [shards(): lax.all_to_all(expert_rows, 'exp', split_axis=1, concat_axis=0, tiled=True)]
    all_gather x1, waiting for transfers between devices: 39 us -> 0.01 us  [shards(): lax.all_gather(mixed_own, 'exp', axis=0, tiled=True)]
    unnamed x1, blocking collectives: 4.01 us -> 29.1 us
    ppermute x0 -> x7, starting transfers between devices: none -> 17.5 us  [shards(): lax.ppermute(ring[-1], 'tok', [(dev, (dev + 1) % 8) for dev in range(8)])]
    reduce_scatter x1, waiting for transfers between devices: 45.4 us -> 52.6 us  [shards(): lax.psum_scatter(lax.dot_general(slope, full_head, (((1,), (1,)), ((), ()...]
  transfers between devices with their start and end apart: 5 -> 11, of which waited for: 5 -> 9; matrix products, arithmetic and copies ran while one was open for 0% -> 14% of each run, Pallas kernels for 0% -> 0%
where the time goes in v1:
time: 644 us; the launch traced here: 643 us
  waiting for transfers between devices  372 us (58%)
  blocking collectives  85.7 us (13%)
  local copies, waits for them, and re-layouts  82.3 us (13%)
  matrix products  36.1 us (6%)
  other arithmetic  28.4 us (4%)
  starting transfers between devices  22.4 us (3%)
  between operations  16.3 us (3%)
    ppermute x7, waiting for transfers between devices, shards(): lax.ppermute(ring[-1], 'tok', [(dev, (dev + 1) % 8) for dev in range(8)])  240 us
    psum x1, waiting for transfers between devices, shards(): router_sum = lax.psum(router_part, ('tok', 'exp'))  79.7 us
    unnamed x53, local copies, waits for them, and re-layouts  78.3 us
    reduce_scatter x1, waiting for transfers between devices, shards(): lax.psum_scatter(lax.dot_general(slope, full_head, (((1,), (1,)), ((), ()...  52.6 us
    psum x1, blocking collectives, shards(): loss_sum = lax.psum(jnp.sum(own_loss), ('tok', 'exp'))  39.8 us
    unnamed x1, blocking collectives  29.1 us
    ppermute x7, starting transfers between devices, shards(): lax.ppermute(ring[-1], 'tok', [(dev, (dev + 1) % 8) for dev in range(8)])  17.5 us
    dot_general x1, matrix products, shards(): lax.dot_general(slope, full_head, (((1,), (1,)), ((), ())), preferred_ele...  17.5 us
  transfers between devices with their start and end apart: 11, of which 9 were waited for; matrix products, arithmetic and copies ran while one was open for 14% of the time, Pallas kernels for 0%

profile of v1, /device:TPU:1, one launch (start us, length us, event | category | flops | bytes accessed | tf_op | source)
XLA Modules:
  0.0 643.3 jit_solution(12575223155650715881)
XLA Ops:
  9.8 44.7 %collective-permute-done = bf16[512,4000]{0,1:T(8,128)(2,1)S(1)} collective-permute-done((bf16[512,4000]{0,1:T(8,128)(2,1)}, bf16[512,4000]{0,1:T(8,128)(2,1)S(1)}, u32[]{:S(2)}, u32[]{:S(2)}) %collective-permute-start) | collective-permute-done | bytes 4096032 | tf_op jit(solution)/shard_map/ppermute | solution.py:31
  59.0 44.4 %collective-permute-done.1 = bf16[512,4000]{0,1:T(8,128)(2,1)S(1)} collective-permute-done((bf16[512,4000]{0,1:T(8,128)(2,1)S(1)}, bf16[512,4000]{0,1:T(8,128)(2,1)S(1)}, u32[]{:S(2)}, u32[]{:S(2)}) %collective-permute-start.1) | collective-permute-done | bytes 4096032 | tf_op jit(solution)/shard_map/ppermute | solution.py:31
  107.9 44.4 %collective-permute-done.2 = bf16[512,4000]{0,1:T(8,128)(2,1)S(1)} collective-permute-done((bf16[512,4000]{0,1:T(8,128)(2,1)S(1)}, bf16[512,4000]{0,1:T(8,128)(2,1)S(1)}, u32[]{:S(2)}, u32[]{:S(2)}) %collective-permute-start.2) | collective-permute-done | bytes 4096032 | tf_op jit(solution)/shard_map/ppermute | solution.py:31
  156.8 44.4 %collective-permute-done.3 = bf16[512,4000]{0,1:T(8,128)(2,1)S(1)} collective-permute-done((bf16[512,4000]{0,1:T(8,128)(2,1)S(1)}, bf16[512,4000]{0,1:T(8,128)(2,1)S(1)}, u32[]{:S(2)}, u32[]{:S(2)}) %collective-permute-start.3) | collective-permute-done | bytes 4096032 | tf_op jit(solution)/shard_map/ppermute | solution.py:31
  205.8 44.4 %collective-permute-done.4 = bf16[512,4000]{0,1:T(8,128)(2,1)} collective-permute-done((bf16[512,4000]{0,1:T(8,128)(2,1)S(1)}, bf16[512,4000]{0,1:T(8,128)(2,1)}, u32[]{:S(2)}, u32[]{:S(2)}) %collective-permute-start.4) | collective-permute-done | bytes 4096032 | tf_op jit(solution)/shard_map/ppermute | solution.py:31
  252.7 8.3 %copy.16 = bf16[1,256,4096]{2,0,1:T(2,128)(2,1)} copy(bf16[1,256,4096]{2,1,0:T(8,128)(2,1)} %param.6) | data formatting | bytes 4194304 | tf_op args[0]
  261.6 13.5 %reduce.1 = bf16[256,4096]{1,0:T(8,128)(2,1)S(1)} reduce(bf16[256,1,4096]{2,1,0:T(2,128)(2,1)} %bitcast.27, bf16[]{:T(256)} %broadcast.108), dimensions={1}, to_apply=%bitcast.23.reduce_sub_computation | reduce | bytes 4194306
  277.9 4.6 all-to-all-start
  282.5 14.9 %collective-permute-done.5 = bf16[512,4000]{0,1:T(8,128)(2,1)} collective-permute-done((bf16[512,4000]{0,1:T(8,128)(2,1)}, bf16[512,4000]{0,1:T(8,128)(2,1)}, u32[]{:S(2)}, u32[]{:S(2)}) %collective-permute-start.5) | collective-permute-done | bytes 4096032 | tf_op jit(solution)/shard_map/ppermute | solution.py:31
  301.4 29.1 %all-reduce = s32[256]{0:T(256)S(1)} all-reduce(s32[256]{0:T(256)S(1)} %dynamic-update-slice), channel_id=1, replica_groups=mesh['tok'=8,'exp'=4] {'exp'}, use_global_device_ids=true, to_apply=%add | all-reduce | flops 256 | bytes 2048
  334.5 6.0 copy_convert_fusion
  344.7 4.4 constant_dynamic-update-slice_fusion.15
  349.0 4.6 constant_dynamic-update-slice_fusion.14
  353.6 4.6 constant_dynamic-update-slice_fusion.13
  375.1 4.3 constant_dynamic-update-slice_fusion.7
  379.4 4.3 constant_dynamic-update-slice_fusion.6
  383.7 4.3 constant_dynamic-update-slice_fusion.5
  399.0 17.1 %fusion.28 = (f32[256]{0:T(256)S(1)}, f32[256,4000]{0,1:T(8,128)}) fusion(bf16[256,4096]{1,0:T(8,128)(2,1)} %all-gather.2.cloned.1.call-done, bf16[8192,4000]{0,1:T(8,128)(2,1)} %constant_dynamic-update-slice_fusion, s32[]{:T(128)S(6)} %select_n.21), kind=kOutput, calls=%fused_computation.63 | convolution fusion | flops 8389632000 | bytes 38962180 | tf_op jit(solution)/shard_map/dot_general | solution.py:35
  416.2 9.9 %pmax.7 = f32[256]{0:T(256)S(1)} all-reduce(f32[256]{0:T(256)S(1)} %get-tuple-element.15), channel_id=1, replica_groups=mesh['tok'=8,'exp'=4] {'exp'}, use_global_device_ids=true, to_apply=%region_3.4 | all-reduce | flops 256 | bytes 2048 | tf_op jit(solution)/shard_map/pmax | solution.py:41
  430.0 6.9 %all-reduce.1 = (f32[256]{0:T(256)S(1)}, f32[256]{0:T(256)S(1)}) all-reduce(f32[256]{0:T(256)S(1)} %get-tuple-element.4, f32[256]{0:T(256)S(1)} %get-tuple-element.3), channel_id=1, replica_groups=mesh['tok'=8,'exp'=4] {'exp'}, use_global_device_ids=true, to_apply=%region_5.6 | all-reduce | flops 512 | bytes 4096 | tf_op jit(solution)/shard_map/psum | solution.py:42
  436.9 17.5 %fusion.4 = bf16[256,4096]{1,0:T(8,128)(2,1)} fusion(bf16[8192,4000]{0,1:T(8,128)(2,1)} %constant_dynamic-update-slice_fusion, s32[]{:T(128)S(6)} %select_n.21, f32[256,4000]{0,1:T(8,128)} %get-tuple-element.16, f32[256]{0:T(256)S(1)} %get-tuple-element.10, s32[256]{0:T(256)S(1)} %all-reduce, s32[4000]{0:T(1024)S(1)} %iota_add_fusion), kind=kOutput, calls=%fused_computation.4 | convolution fusion | flops 8395800576 | bytes 38979204 | tf_op jit(solution)/shard_map/dot_general | solution.py:53
  454.4 52.6 %reduce-scatter.2.cloned.1.call-done = bf16[64,4096]{1,0:T(8,128)(2,1)} async-done(((bf16[256,4096]{1,0:T(8,128)(2,1)}), bf16[64,4096]{1,0:T(8,128)(2,1)}) %reduce-scatter.2.cloned.1.call-update) | async-done | bytes 524304 | tf_op jit(solution)/shard_map/reduce_scatter | solution.py:52
  514.1 39.8 %psum.31 = f32[]{:T(128)} all-reduce(f32[]{:T(128)} %get-tuple-element.7), channel_id=1, replica_groups=mesh['tok'=8,'exp'=4] {'tok','exp'}, use_global_device_ids=true, to_apply=%region_13.14 | all-reduce | flops 1 | bytes 8 | tf_op jit(solution)/shard_map/psum | solution.py:48
  554.5 79.7 %all-reduce.4.cloned.1.call-done = f32[4096,4]{0,1:T(4,128)} async-done(((f32[4096,4]{0,1:T(4,128)}), f32[4096,4]{0,1:T(4,128)}) %all-reduce.4.cloned.1.call-update) | async-done | bytes 65552 | tf_op jit(solution)/shard_map/psum | solution.py:64
  (78 shorter events, 78.1 us)
Async XLA Ops:
  7.2 323.4 %copy-start = (bf16[64,4096]{1,0:T(8,128)(2,1)S(1)}, bf16[64,4096]{1,0:T(8,128)(2,1)}, u32[]{:S(2)}) copy-start(bf16[64,4096]{1,0:T(8,128)(2,1)} %param.7) | copy-start | bytes 1572868
  7.2 47.4 %collective-permute-start = (bf16[512,4000]{0,1:T(8,128)(2,1)}, bf16[512,4000]{0,1:T(8,128)(2,1)S(1)}, u32[]{:S(2)}, u32[]{:S(2)}) collective-permute-start(bf16[512,4000]{0,1:T(8,128)(2,1)} %param.11), channel_id=1, source_target_pairs={{0,4},{4,8},{8,12},{12,16},{16,20},{20,24},{24,28},{28,0},{1,5},{5... | collective-permute-start | bytes 12288008 | tf_op jit(solution)/shard_map/ppermute | solution.py:31
  54.5 2.1 copy-start.3
  56.6 46.8 %collective-permute-start.1 = (bf16[512,4000]{0,1:T(8,128)(2,1)S(1)}, bf16[512,4000]{0,1:T(8,128)(2,1)S(1)}, u32[]{:S(2)}, u32[]{:S(2)}) collective-permute-start(bf16[512,4000]{0,1:T(8,128)(2,1)S(1)} %collective-permute-done), channel_id=1, source_target_pairs={{0,4},{4,8},{8,12},{12,16},{16,20},{20,24},{24,28},{28,0},{1,5},{5... | collective-permute-start | bytes 12288008 | tf_op jit(solution)/shard_map/ppermute | solution.py:31
  105.4 46.9 %collective-permute-start.2 = (bf16[512,4000]{0,1:T(8,128)(2,1)S(1)}, bf16[512,4000]{0,1:T(8,128)(2,1)S(1)}, u32[]{:S(2)}, u32[]{:S(2)}) collective-permute-start(bf16[512,4000]{0,1:T(8,128)(2,1)S(1)} %collective-permute-done.1), channel_id=1, source_target_pairs={{0,4},{4,8},{8,12},{12,16},{16,20},{20,24},{24,28},{28,0},{1,5},{5... | collective-permute-start | bytes 12288008 | tf_op jit(solution)/shard_map/ppermute | solution.py:31
  154.3 46.9 %collective-permute-start.3 = (bf16[512,4000]{0,1:T(8,128)(2,1)S(1)}, bf16[512,4000]{0,1:T(8,128)(2,1)S(1)}, u32[]{:S(2)}, u32[]{:S(2)}) collective-permute-start(bf16[512,4000]{0,1:T(8,128)(2,1)S(1)} %collective-permute-done.2), channel_id=1, source_target_pairs={{0,4},{4,8},{8,12},{12,16},{16,20},{20,24},{24,28},{28,0},{1,5},{5... | collective-permute-start | bytes 12288008 | tf_op jit(solution)/shard_map/ppermute | solution.py:31
  201.2 2.1 copy-start.9
  203.3 46.9 %collective-permute-start.4 = (bf16[512,4000]{0,1:T(8,128)(2,1)S(1)}, bf16[512,4000]{0,1:T(8,128)(2,1)}, u32[]{:S(2)}, u32[]{:S(2)}) collective-permute-start(bf16[512,4000]{0,1:T(8,128)(2,1)S(1)} %collective-permute-done.3), channel_id=1, source_target_pairs={{0,4},{4,8},{8,12},{12,16},{16,20},{20,24},{24,28},{28,0},{1,5},{5... | collective-permute-start | bytes 12288008 | tf_op jit(solution)/shard_map/ppermute | solution.py:31
  250.2 47.3 %collective-permute-start.5 = (bf16[512,4000]{0,1:T(8,128)(2,1)}, bf16[512,4000]{0,1:T(8,128)(2,1)}, u32[]{:S(2)}, u32[]{:S(2)}) collective-permute-start(bf16[512,4000]{0,1:T(8,128)(2,1)} %collective-permute-done.4), channel_id=1, source_target_pairs={{0,4},{4,8},{8,12},{12,16},{16,20},{20,24},{24,28},{28,0},{1,5},{5... | collective-permute-start | bytes 12288008 | tf_op jit(solution)/shard_map/ppermute | solution.py:31
  275.1 24.8 %copy-start.14 = (u32[32]{0:T(128)S(1)}, u32[32]{0:T(128)}, u32[]{:S(2)}) copy-start(u32[32]{0:T(128)} %constant.58) | copy-start | bytes 388
  275.1 26.1 %copy-start.13 = (s32[64]{0:T(128)S(1)}, s32[64]{0:T(128)}, u32[]{:S(2)}) copy-start(s32[64]{0:T(128)} %param.10) | copy-start | bytes 772
  275.1 55.5 %copy-start.12 = (s32[64,2]{0,1:T(2,128)S(1)}, s32[64,2]{0,1:T(2,128)}, u32[]{:S(2)}) copy-start(s32[64,2]{0,1:T(2,128)} %param.9) | copy-start | bytes 1540
  275.1 55.5 %copy-start.11 = (f32[4096,4]{0,1:T(4,128)S(1)}, f32[4096,4]{0,1:T(4,128)}, u32[]{:S(2)}) copy-start(f32[4096,4]{0,1:T(4,128)} %param.8) | copy-start | bytes 196612
  277.9 53.2 %all-to-all-start = ((bf16[4,2,131072]{2,1,0:T(2,128)(2,1)}), bf16[4,2,131072]{2,1,0:T(2,128)(2,1)S(1)}, u32[]{:S(2)}, u32[]{:S(2)}) async-start(bf16[4,2,131072]{2,1,0:T(2,128)(2,1)} %reshape.110), calls=%async_computation | async-start | bytes 4194304 | tf_op jit(solution)/shard_map/all_to_all | solution.py:21
  282.5 116.5 %all-gather.2.cloned.1.call-start = ((), (), s32[]{:S(2)}) async-start(), calls=%async_computation.2 | async-start | bytes 2621440 | tf_op jit(solution)/shard_map/all_gather | solution.py:25
  297.5 47.2 %collective-permute-start.6 = (bf16[512,4000]{0,1:T(8,128)(2,1)}, bf16[512,4000]{0,1:T(8,128)(2,1)}, u32[]{:S(2)}, u32[]{:S(2)}) collective-permute-start(bf16[512,4000]{0,1:T(8,128)(2,1)} %collective-permute-done.5), channel_id=1, source_target_pairs={{0,4},{4,8},{8,12},{12,16},{16,20},{20,24},{24,28},{28,0},{1,5},{5... | collective-permute-start | bytes 12288008 | tf_op jit(solution)/shard_map/ppermute | solution.py:31
  341.9 165.2 %reduce-scatter.2.cloned.1.call-start = ((), (), s32[]{:S(2)}) async-start(), calls=%async_computation.3 | async-start | bytes 2621440 | tf_op jit(solution)/shard_map/reduce_scatter | solution.py:52
  353.6 4.6 copy-start.10
  358.2 3.7 copy-start.8
  361.9 3.6 copy-start.6
  365.5 3.7 copy-start.4
  369.2 3.7 copy-start.2
  454.4 179.8 %all-reduce.4.cloned.1.call-start = ((), (), s32[]{:S(2)}) async-start(), calls=%async_computation.4 | async-start | bytes 131072 | tf_op jit(solution)/shard_map/psum | solution.py:64
  507.1 2.3 copy-start.1
  (2 other events, 4.0 us)
Sparse Core Ops, SparseCore 0:
  342.0 45.9 all-gather.1
  454.5 52.5 reduce-scatter.1
  513.2 120.9 all-reduce.3
